TPU v7x, 128 devices: a whole 4x4x4 slice. The times are simulated.
128 devices in a mesh: zero: 32 (over y, x, core), width: 4 (over z).
Axes of the slice: x: 4, y: 4, z: 4, core: 2. Of those that a mesh axis runs over, the one named last changes fastest.
Arguments:
- train_query: bfloat16 [3584, 4096], P('zero', 'width'), may hold values from -0.09375 to 0.09375
- low_query: bfloat16 [3584, 32], P('zero'), may hold values from -0.09375 to 0.09375
- high_query: bfloat16 [32, 4096], P(None, 'width'), may hold values from -1 to 1
- train_key: bfloat16 [3584, 2048], P('zero', 'width'), may hold values from -0.09375 to 0.09375
- low_key: bfloat16 [3584, 32], P('zero'), may hold values from -0.09375 to 0.09375
- high_key: bfloat16 [32, 2048], P(None, 'width'), may hold values from -1 to 1
- train_value: bfloat16 [3584, 2048], P('zero', 'width'), may hold values from -0.09375 to 0.09375
- low_value: bfloat16 [3584, 32], P('zero'), may hold values from -0.09375 to 0.09375
- high_value: bfloat16 [32, 2048], P(None, 'width'), may hold values from -1 to 1
- train_mixed: bfloat16 [4096, 3584], P('width', 'zero'), may hold values from -0.09375 to 0.09375
- low_mixed: bfloat16 [4096, 32], P('width'), may hold values from -0.09375 to 0.09375
- high_mixed: bfloat16 [32, 3584], P(None, 'zero'), may hold values from -1 to 1
- norm_train: float32 [3584], P(('zero', 'width')), may hold values from 0.25 to 1.75
- norm_step: float32 [3584], P(('zero', 'width')), may hold values from -0.3 to 0.3
Outputs:
- ready_query: bfloat16 [4096, 3584], P('width')
- ready_key: bfloat16 [2048, 3584], P('width')
- ready_value: bfloat16 [2048, 3584], P('width')
- ready_mixed: bfloat16 [3584, 4096], P(None, 'width')
- serve_norm: bfloat16 [3584], replicated
All inputs are finite; a program needn't handle non-finite values.
Results may differ from a plain program's by a relative error of at most 0.001.
Values may be sent and summed in bfloat16 or wider, within the bound.
No kernel may reach another device: no remote copies, remote signals or barrier semaphores. Data moves between devices by JAX's collectives and lax.ppermute only.
A program may use at most 128 MiB of HBM per device.

v0:
```python
import jax
import jax.numpy as jnp
from jax import lax
from jax.sharding import Mesh
from jax.sharding import PartitionSpec as P

ZERO = ("zero_0", "zero_1", "zero_2")
ZERO_WIDTH = ("zero_0", "zero_1", "zero_2", "width")
mix_rate = 0.5


def turned_gather(arrays, axis, dims):
    turned = [jnp.moveaxis(a, dim, 0) for a, dim in zip(arrays, dims)]
    both = jnp.concatenate([t.reshape(len(t), -1) for t in turned], axis=1)
    whole, at, done = (lax.all_gather(both, axis, axis=0, tiled=True), 0, [])
    for t, dim in zip(turned, dims):
        piece = whole[:, at : at + t[0].size].reshape(-1, *t.shape[1:])
        done.append(jnp.moveaxis(piece, 0, dim))
        at += t[0].size
    return tuple(done)


def joined_along(pieces, dim):
    lengths = list(pieces.shape[1:])
    lengths[dim] *= pieces.shape[0]
    return jnp.moveaxis(pieces, 0, dim).reshape(lengths)


def gather_in_order(array, axes, sequence):
    pieces = array
    for k in sequence:
        pieces = lax.all_gather(pieces, axes[k])
    done = sequence[::-1]
    back = [done.index(k) for k in range(len(axes))]
    pieces = pieces.transpose(*back, *range(len(axes), pieces.ndim))
    return pieces.reshape(-1, *array.shape)


def gathered_by_axis(array, axes, sequence, dim):
    return joined_along(gather_in_order(array, axes, sequence), dim)


def body(
    train_query,
    low_query,
    high_query,
    train_key,
    low_key,
    high_key,
    train_value,
    low_value,
    high_value,
    train_mixed,
    low_mixed,
    high_mixed,
    norm_train,
    norm_step,
):
    latest_query = train_query.astype(jnp.float32) + mix_rate * jnp.dot(
        low_query, high_query, preferred_element_type=jnp.float32
    )
    latest_key = train_key.astype(jnp.float32) + mix_rate * jnp.dot(
        low_key, high_key, preferred_element_type=jnp.float32
    )
    latest_value = train_value.astype(jnp.float32) + mix_rate * jnp.dot(
        low_value, high_value, preferred_element_type=jnp.float32
    )
    latest_mixed = train_mixed.astype(jnp.float32) + mix_rate * jnp.dot(
        low_mixed, high_mixed, preferred_element_type=jnp.float32
    )
    narrow_query, narrow_key, narrow_value, narrow_mixed = (
        latest_query.astype(jnp.bfloat16),
        latest_key.astype(jnp.bfloat16),
        latest_value.astype(jnp.bfloat16),
        latest_mixed.astype(jnp.bfloat16),
    )
    ready_query, ready_key, ready_value, ready_mixed = turned_gather(
        (narrow_query, narrow_key, narrow_value, narrow_mixed), ZERO, (0, 0, 0, 1)
    )
    ready_query, ready_key, ready_value, ready_mixed = (
        ready_query.T,
        ready_key.T,
        ready_value.T,
        ready_mixed.T,
    )
    serve_norm = gathered_by_axis(
        (norm_train + norm_step).astype(jnp.bfloat16), ZERO_WIDTH, (0, 1, 3, 2), 0
    )
    return (ready_query, ready_key, ready_value, ready_mixed, serve_norm)


def solution(mesh):
    torus = Mesh(
        mesh.devices.reshape(4, 4, 2, mesh.shape["width"]), ("zero_0", "zero_1", "zero_2", "width")
    )
    return jax.shard_map(
        body,
        mesh=torus,
        in_specs=(
            P(ZERO, "width"),
            P(ZERO, None),
            P(None, "width"),
            P(ZERO, "width"),
            P(ZERO, None),
            P(None, "width"),
            P(ZERO, "width"),
            P(ZERO, None),
            P(None, "width"),
            P("width", ZERO),
            P("width", None),
            P(None, ZERO),
            P(ZERO_WIDTH),
            P(ZERO_WIDTH),
        ),
        out_specs=(P("width", None), P("width", None), P("width", None), P(None, "width"), P()),
        check_vma=False,
    )
```

profile of v0, /device:TPU:1, one launch (start us, length us, event | category | flops | bytes accessed | tf_op | source)
XLA Modules:
  0.0 148.0 jit_solution(1790377427683227908)
XLA Ops:
  7.2 0.0 copy-start
  7.2 0.0 copy-start.3
  7.2 0.0 all-gather.7.cloned.1.call-start
  7.3 0.8 copy-done
  8.0 1.2 fusion.3
  9.2 1.2 fusion.4
  10.5 1.1 fusion.7
  11.6 1.1 fusion.8
  12.8 0.9 pad_maximum_fusion
  13.7 0.0 all-gather.7.cloned.1.call-update
  13.7 0.6 dynamic-slice
  15.0 0.2 dynamic-update-slice
  15.2 9.5 %all-reduce = bf16[112]{0:T(256)(128)(2,1)S(1)} all-reduce(bf16[112]{0:T(256)(128)(2,1)S(1)} %dynamic-update-slice), channel_id=2, replica_groups=mesh['zero_0'=4,'zero_1'=4,'zero_2'=2,'width'=4] {'zero_0'}, use_global_device_ids=true, to_apply=%add | all-reduce | flops 112 | bytes 448
  24.8 0.1 reshape.17
  24.8 8.1 %all-gather.4 = bf16[4,4,28]{2,1,0:T(4,128)(2,1)S(1)} all-gather(bf16[1,4,28]{2,1,0:T(4,128)(2,1)S(1)} %reshape.17), channel_id=3, replica_groups=mesh['zero_0'=4,'zero_1'=4,'zero_2'=2,'width'=4] {'zero_1'}, dimensions={0}, use_global_device_ids=true | all-gather | bytes 1120 | tf_op jit(solution)/shard_map/all_gather | solution.py:32
  33.0 11.5 %all-gather.2 = bf16[16,4,28]{2,1,0:T(4,128)(2,1)S(1)} all-gather(bf16[4,4,28]{2,1,0:T(4,128)(2,1)S(1)} %all-gather.4), channel_id=4, replica_groups=mesh['zero_0'=4,'zero_1'=4,'zero_2'=2,'width'=4] {'width'}, dimensions={0}, use_global_device_ids=true | all-gather | bytes 4480 | tf_op jit(solution)/shard_map/all_gather | solution.py:32
  44.4 7.5 %all-gather.3 = bf16[8,4,4,28]{3,2,1,0:T(4,128)(2,1)S(1)} all-gather(bf16[4,4,4,28]{3,2,1,0:T(4,128)(2,1)S(1)} %bitcast.24), channel_id=5, replica_groups=mesh['zero_0'=4,'zero_1'=4,'zero_2'=2,'width'=4] {'zero_2'}, dimensions={0}, use_global_device_ids=true | all-gather | bytes 10752 | tf_op jit(solution)/shard_map/all_gather | solution.py:32
  52.0 0.7 reshape_reshape.3
  52.7 49.3 %all-gather.7.cloned.1.call-done = bf16[3584,3072]{1,0:T(8,128)(2,1)} async-done(((bf16[112,3072]{1,0:T(8,128)(2,1)}), bf16[3584,3072]{1,0:T(8,128)(2,1)}) %all-gather.7.cloned.1.call-update) | async-done | bytes 22020112 | tf_op jit(solution)/shard_map/all_gather | solution.py:15
  102.0 10.7 %fusion.9 = (bf16[3584,1024]{1,0:T(8,128)(2,1)}, bf16[1024,3584]{0,1:T(8,128)(2,1)}) fusion(bf16[3584,3072]{1,0:T(8,128)(2,1)} %all-gather.7.cloned.1.call-done), kind=kLoop, calls=%fused_computation.19 | loop fusion | bytes 29360128 | tf_op jit(solution)/shard_map/slice | solution.py:17
  112.7 9.9 %copy.27 = bf16[1024,3584]{1,0:T(8,128)(2,1)} copy(bf16[1024,3584]{0,1:T(8,128)(2,1)} %get-tuple-element.21) | data formatting | bytes 14680064
  122.6 6.7 %slice_bitcast_fusion.1 = (bf16[512,3584]{0,1:T(8,128)(2,1)}, bf16[512,3584]{0,1:T(8,128)(2,1)}) fusion(bf16[3584,3072]{1,0:T(8,128)(2,1)} %all-gather.7.cloned.1.call-done), kind=kLoop, calls=%fused_computation.1 | loop fusion | bytes 14680064 | tf_op jit(solution)/shard_map/transpose | solution.py:83
  129.3 5.9 %copy.28 = bf16[512,3584]{1,0:T(8,128)(2,1)} copy(bf16[512,3584]{0,1:T(8,128)(2,1)} %get-tuple-element.23) | data formatting | bytes 7340032
  135.2 5.9 %copy.29 = bf16[512,3584]{1,0:T(8,128)(2,1)} copy(bf16[512,3584]{0,1:T(8,128)(2,1)} %get-tuple-element.22) | data formatting | bytes 7340032
  (8 shorter events, 0.0 us)
Async XLA Ops:
  7.2 0.8 copy-start
  7.2 6.5 %copy-start.3 = (u32[128]{0:T(128)S(1)}, u32[128]{0:T(128)}, u32[]{:S(2)}) copy-start(u32[128]{0:T(128)} %constant.16) | copy-start | bytes 1540
  7.2 7.8 %copy-start.1 = (f32[28]{0:T(128)S(1)}, f32[28]{0:T(128)}, u32[]{:S(2)}) copy-start(f32[28]{0:T(128)} %param.26) | copy-start | bytes 340
  7.2 7.8 %copy-start.2 = (f32[28]{0:T(128)S(1)}, f32[28]{0:T(128)}, u32[]{:S(2)}) copy-start(f32[28]{0:T(128)} %param.27) | copy-start | bytes 340
  7.2 94.8 %all-gather.7.cloned.1.call-start = ((), (), s32[]{:S(2)}) async-start(), calls=%async_computation | async-start | bytes 22708224 | tf_op jit(solution)/shard_map/all_gather | solution.py:15
Sparse Core Ops, SparseCore 0:
  13.8 88.1 all-gather.6
where the time goes:
time: 149 us; the launch traced here: 148 us
  waiting for transfers between devices  49.3 us (33%)
  local copies, waits for them, and re-layouts  41.6 us (28%)
  blocking collectives  36.6 us (25%)
  between operations  14.8 us (10%)
  matrix products  4.73 us (3%)
    all_gather x1, waiting for transfers between devices, turned_gather(): whole, at, done = (lax.all_gather(both, axis, axis=0, tiled=True), 0, [])  49.3 us
    all_gather x3, blocking collectives, gather_in_order(): pieces = lax.all_gather(pieces, axes[k])  27.1 us
    unnamed x15, local copies, waits for them, and re-layouts  23.4 us
    slice x1, local copies, waits for them, and re-layouts, turned_gather(): piece = whole[:, at:at + t[0].size].reshape(-1, *t.shape[1:])  10.7 us
    unnamed x1, blocking collectives  9.52 us
    transpose x1, local copies, waits for them, and re-layouts, body(): ready_query, ready_key, ready_value, ready_mixed = (ready_query.T, ready_...  6.68 us
  transfers between devices with their start and end apart: 1, of which 1 were waited for; matrix products, arithmetic and copies ran while one was open for 1% of the time, Pallas kernels for 0%

commit v1 on v0

--- a/solution.py
+++ b/solution.py
@@ -3,6 +3,7 @@
 from jax import lax
 from jax.sharding import Mesh
 from jax.sharding import PartitionSpec as P
+from jax.lax import all_to_all, psum
 
 ZERO = ("zero_0", "zero_1", "zero_2")
 ZERO_WIDTH = ("zero_0", "zero_1", "zero_2", "width")
@@ -12,7 +13,19 @@
 def turned_gather(arrays, axis, dims):
     turned = [jnp.moveaxis(a, dim, 0) for a, dim in zip(arrays, dims)]
     both = jnp.concatenate([t.reshape(len(t), -1) for t in turned], axis=1)
-    whole, at, done = (lax.all_gather(both, axis, axis=0, tiled=True), 0, [])
+    whole, at, done = (
+        jnp.concatenate(
+            all_to_all(
+                jnp.stack([both for _ in range(psum(1, axis_name=axis))]),
+                axis_name=axis,
+                split_axis=0,
+                concat_axis=0,
+            ),
+            axis=0,
+        ),
+        0,
+        [],
+    )
     for t, dim in zip(turned, dims):
         piece = whole[:, at : at + t[0].size].reshape(-1, *t.shape[1:])
         done.append(jnp.moveaxis(piece, 0, dim))

time: 149 us -> 360 us (2.42)
  blocking collectives: 36.6 us -> 291 us
  waiting for transfers between devices: 49.3 us -> 0.01 us
  between operations: 14.8 us -> 1.39 us
  local copies, waits for them, and re-layouts: 41.6 us -> 50.9 us
  starting transfers between devices: 0.04 us -> 8.76 us
    unnamed x1, blocking collectives: 9.52 us -> 260 us
    all_gather x1 -> x0, waiting for transfers between devices: 49.3 us -> none  [turned_gather(): whole, at, done = (lax.all_gather(both, axis, axis=0, tiled=True), 0, [])]
    another operation x0 -> x1, local copies, waits for them, and re-layouts: none -> 9.21 us  [turned_gather(): jnp.stack([both for _ in range(psum(1, axis_name=axis))])]
    all_to_all x0 -> x1, starting transfers between devices: none -> 8.76 us  [turned_gather(): all_to_all(jnp.stack([both for _ in range(psum(1, axis_name=axis))]), axi...]
    all_gather x3, blocking collectives: 27.1 us -> 31.4 us  [gather_in_order(): pieces = lax.all_gather(pieces, axes[k])]
    unnamed x15 -> x17, local copies, waits for them, and re-layouts: 23.4 us -> 23.6 us
  transfers between devices with their start and end apart: 1 -> 1, of which waited for: 1 -> 0; matrix products, arithmetic and copies ran while one was open for 1% -> 0% of each run, Pallas kernels for 0% -> 0%
where the time goes in v1:
time: 360 us; the launch traced here: 357 us
  blocking collectives  291 us (81%)
  local copies, waits for them, and re-layouts  50.9 us (14%)
  starting transfers between devices  8.76 us (2%)
  matrix products  4.73 us (1%)
    unnamed x1, blocking collectives  260 us
    all_gather x3, blocking collectives, gather_in_order(): pieces = lax.all_gather(pieces, axes[k])  31.4 us
    unnamed x17, local copies, waits for them, and re-layouts  23.6 us
    slice x1, local copies, waits for them, and re-layouts, turned_gather(): piece = whole[:, at:at + t[0].size].reshape(-1, *t.shape[1:])  10.7 us
    another operation x1, local copies, waits for them, and re-layouts, turned_gather(): jnp.stack([both for _ in range(psum(1, axis_name=axis))])  9.21 us
    all_to_all x1, starting transfers between devices, turned_gather(): all_to_all(jnp.stack([both for _ in range(psum(1, axis_name=axis))]), axi...  8.76 us
  transfers between devices with their start and end apart: 1, of which 0 were waited for; matrix products, arithmetic and copies ran while one was open for 0% of the time, Pallas kernels for 0%

profile of v1, /device:TPU:1, one launch (start us, length us, event | category | flops | bytes accessed | tf_op | source)
XLA Modules:
  0.0 357.0 jit_solution(13324261744216593564)
XLA Ops:
  0.6 0.0 copy-start
  0.6 0.8 copy-done
  1.5 1.2 fusion.3
  2.7 1.2 fusion.4
  3.9 1.1 fusion.7
  5.1 1.1 fusion.8
  6.2 0.1 pad_maximum_fusion
  6.3 9.2 %stack.2 = bf16[32,112,3072]{2,1,0:T(8,128)(2,1)} broadcast(bf16[112,3072]{1,0:T(8,128)(2,1)S(1)} %pad_maximum_fusion), dimensions={1,2} | broadcast | bytes 22708224 | tf_op jit(solution)/shard_map/stack | solution.py:19
  15.5 8.8 %all-to-all-start = ((bf16[32,112,3072]{2,1,0:T(8,128)(2,1)}), bf16[32,112,3072]{2,1,0:T(8,128)(2,1)}, u32[]{:S(2)}, u32[]{:S(2)}) async-start(bf16[32,112,3072]{2,1,0:T(8,128)(2,1)} %stack.2), calls=%async_computation | async-start | bytes 44040192 | tf_op jit(solution)/shard_map/all_to_all | solution.py:18
  24.3 0.0 copy-done.4
  24.3 0.6 dynamic-slice
  25.6 0.2 dynamic-update-slice
  25.8 259.8 %all-reduce = bf16[112]{0:T(256)(128)(2,1)S(1)} all-reduce(bf16[112]{0:T(256)(128)(2,1)S(1)} %dynamic-update-slice), channel_id=2, replica_groups=mesh['zero_0'=4,'zero_1'=4,'zero_2'=2,'width'=4] {'zero_0'}, use_global_device_ids=true, to_apply=%add | all-reduce | flops 112 | bytes 448
  285.6 0.1 reshape.23
  285.7 15.3 %all-gather.4 = bf16[4,4,28]{2,1,0:T(4,128)(2,1)S(1)} all-gather(bf16[1,4,28]{2,1,0:T(4,128)(2,1)S(1)} %reshape.23), channel_id=3, replica_groups=mesh['zero_0'=4,'zero_1'=4,'zero_2'=2,'width'=4] {'zero_1'}, dimensions={0}, use_global_device_ids=true | all-gather | bytes 1120 | tf_op jit(solution)/shard_map/all_gather | solution.py:45
  301.0 10.3 %all-gather.2 = bf16[16,4,28]{2,1,0:T(4,128)(2,1)S(1)} all-gather(bf16[4,4,28]{2,1,0:T(4,128)(2,1)S(1)} %all-gather.4), channel_id=4, replica_groups=mesh['zero_0'=4,'zero_1'=4,'zero_2'=2,'width'=4] {'width'}, dimensions={0}, use_global_device_ids=true | all-gather | bytes 4480 | tf_op jit(solution)/shard_map/all_gather | solution.py:45
  311.3 5.8 %all-gather.3 = bf16[8,4,4,28]{3,2,1,0:T(4,128)(2,1)S(1)} all-gather(bf16[4,4,4,28]{3,2,1,0:T(4,128)(2,1)S(1)} %bitcast.25), channel_id=5, replica_groups=mesh['zero_0'=4,'zero_1'=4,'zero_2'=2,'width'=4] {'zero_2'}, dimensions={0}, use_global_device_ids=true | all-gather | bytes 10752 | tf_op jit(solution)/shard_map/all_gather | solution.py:45
  317.1 0.7 reshape_reshape.3
  317.8 0.0 all-to-all-done
  317.8 10.7 %fusion.9 = (bf16[3584,1024]{1,0:T(8,128)(2,1)}, bf16[1024,3584]{0,1:T(8,128)(2,1)}) fusion(bf16[3584,3072]{1,0:T(8,128)(2,1)} %bitcast.1), kind=kLoop, calls=%fused_computation.19 | loop fusion | bytes 29360128 | tf_op jit(solution)/shard_map/slice | solution.py:30
  328.5 6.7 %slice_bitcast_fusion.1 = (bf16[512,3584]{0,1:T(8,128)(2,1)}, bf16[512,3584]{0,1:T(8,128)(2,1)}) fusion(bf16[3584,3072]{1,0:T(8,128)(2,1)} %bitcast.1), kind=kLoop, calls=%fused_computation.1 | loop fusion | bytes 14680064 | tf_op jit(solution)/shard_map/transpose | solution.py:96
  335.2 9.9 %copy.27 = bf16[1024,3584]{1,0:T(8,128)(2,1)} copy(bf16[1024,3584]{0,1:T(8,128)(2,1)} %get-tuple-element.21) | data formatting | bytes 14680064
  345.2 5.9 %copy.28 = bf16[512,3584]{1,0:T(8,128)(2,1)} copy(bf16[512,3584]{0,1:T(8,128)(2,1)} %get-tuple-element.23) | data formatting | bytes 7340032
  351.1 5.9 %copy.29 = bf16[512,3584]{1,0:T(8,128)(2,1)} copy(bf16[512,3584]{0,1:T(8,128)(2,1)} %get-tuple-element.22) | data formatting | bytes 7340032
  (10 shorter events, 0.0 us)
Async XLA Ops:
  0.6 0.8 copy-start
  15.5 8.8 %copy-start.4 = (u32[128]{0:T(128)S(1)}, u32[128]{0:T(128)}, u32[]{:S(2)}) copy-start(u32[128]{0:T(128)} %constant.16) | copy-start | bytes 1540
  15.5 10.0 %copy-start.2 = (f32[28]{0:T(128)S(1)}, f32[28]{0:T(128)}, u32[]{:S(2)}) copy-start(f32[28]{0:T(128)} %param.26) | copy-start | bytes 340
  15.5 10.0 %copy-start.3 = (f32[28]{0:T(128)S(1)}, f32[28]{0:T(128)}, u32[]{:S(2)}) copy-start(f32[28]{0:T(128)} %param.27) | copy-start | bytes 340
  15.5 302.3 %all-to-all-start = ((bf16[32,112,3072]{2,1,0:T(8,128)(2,1)}), bf16[32,112,3072]{2,1,0:T(8,128)(2,1)}, u32[]{:S(2)}, u32[]{:S(2)}) async-start(bf16[32,112,3072]{2,1,0:T(8,128)(2,1)} %stack.2), calls=%async_computation | async-start | bytes 44040192 | tf_op jit(solution)/shard_map/all_to_all | solution.py:18
  351.1 5.9 %copy-start.1 = (bf16[32,1024]{1,0:T(8,128)(2,1)S(1)}, bf16[32,1024]{1,0:T(8,128)(2,1)}, u32[]{:S(2)}) copy-start(bf16[32,1024]{1,0:T(8,128)(2,1)} %param.16) | copy-start | bytes 196612
